TPU v7x, 32 devices: a whole 2x2x4 slice. The times are simulated.
32 devices in a mesh: cluster: 4 (over y, x), member: 8 (over z, core).
Axes of the slice: x: 2, y: 2, z: 4, core: 2. Of those that a mesh axis runs over, the one named last changes fastest.
Arguments:
- embeddings: bfloat16 [8192, 4096], P(('cluster', 'member')), may hold values from -15 to 15, as said below
- start_basis: bfloat16 [4096, 512], P(('cluster', 'member')), may hold values from -6 to 6
- cluster_ids: int32 [8192], P(('cluster', 'member')), may hold values from 0 to 7
- valid_counts: int32 [4], P('cluster'), may hold values from 512 to 2048
Outputs:
- subspace: float32 [4096, 512], P(('cluster', 'member'))
- nearest: float32 [8192], P(('cluster', 'member'))
Inputs may be any that keep to these rules, and one draw needn't show every extreme that they name: `embeddings`: Real-valued entries.
All inputs are finite; a program needn't handle non-finite values.
Results may differ from a plain program's by a relative error of at most 0.0042.
Values may be sent and summed in bfloat16 or wider, within the bound.
No kernel may reach another device: no remote copies, remote signals or barrier semaphores. Data moves between devices by JAX's collectives and lax.ppermute only.
A program may use at most 64 MiB of HBM per device.

v0:
```python
import math
import jax
import jax.numpy as jnp
from jax import lax
from jax.sharding import PartitionSpec as P

D = 4096
ITERS = 2
EPS = 1e-06


def spread_basis(local_rows):
    return lax.all_gather(local_rows, ("cluster", "member"), axis=0, tiled=True)


def reduce_image(centered, projected):
    return lax.psum_scatter(
        lax.dot_general(
            centered, projected, (((0,), (0,)), ((), ())), preferred_element_type=jnp.float32
        ),
        ("cluster", "member"),
        scatter_dimension=0,
        tiled=True,
    )


def body(embeddings, start_basis, cluster_ids, valid_counts):
    row_count = embeddings.shape[0]
    total_rows = row_count * lax.axis_size(("cluster", "member"))
    ones_row = jnp.ones((1, row_count), jnp.bfloat16)
    column_sums = jnp.dot(ones_row, embeddings, preferred_element_type=jnp.float32)[0]
    average = lax.psum(column_sums, ("cluster", "member")) / total_rows
    centered = (embeddings.astype(jnp.float32) - average).astype(jnp.bfloat16)
    basis_full = spread_basis(start_basis)
    orthonormal = None
    for sweep in range(ITERS):
        projected = jnp.dot(centered, basis_full, preferred_element_type=jnp.float32).astype(
            jnp.bfloat16
        )
        image = reduce_image(centered, projected) / total_rows
        local_gram = jnp.dot(image.T, image, precision=lax.Precision.HIGHEST)
        gram = lax.psum(local_gram, ("cluster", "member"))
        lower = jnp.linalg.cholesky(gram)
        orthonormal = jax.scipy.linalg.solve_triangular(lower, image.T, lower=True).T
        basis_full = spread_basis(orthonormal.astype(jnp.bfloat16))
    subspace = orthonormal * math.sqrt(D)
    coords = jnp.dot(centered, basis_full, preferred_element_type=jnp.float32)
    unit = (coords * lax.rsqrt(jnp.sum(coords * coords, axis=1, keepdims=True) + EPS)).astype(
        jnp.bfloat16
    )
    label_values = cluster_ids.astype(jnp.bfloat16)
    limit = valid_counts[0]
    own_index = lax.axis_index("member") * row_count + jnp.arange(row_count, dtype=jnp.int32)
    initial = jnp.full((row_count,), -1.0, jnp.float32)
    piece_units = lax.all_gather(unit, "member", axis=0, tiled=True)
    piece_labels = lax.all_gather(label_values, "member", axis=0, tiled=True)
    scores = lax.dot_general(
        unit, piece_units, (((1,), (1,)), ((), ())), preferred_element_type=jnp.float32
    )
    others = jnp.arange(piece_units.shape[0], dtype=jnp.int32)
    allowed = (
        (label_values[:, None] == piece_labels[None, :])
        & (others[None, :] < limit)
        & (others[None, :] != own_index[:, None])
    )
    nearest = jnp.maximum(initial, jnp.max(jnp.where(allowed, scores, -1.0), axis=1))
    return (subspace, nearest)


def solution(mesh):
    placed = (
        P(("cluster", "member"), None),
        P(("cluster", "member"), None),
        P(("cluster", "member")),
        P("cluster"),
    )
    return jax.shard_map(
        body,
        mesh=mesh,
        in_specs=placed,
        out_specs=(P(("cluster", "member"), None), P(("cluster", "member"))),
        check_vma=False,
    )
```

profile of v0, /device:TPU:0, one launch (start us, length us, event | category | flops | bytes accessed | tf_op | source)
XLA Modules:
  0.0 1155.7 jit_solution(3383755361846079378)
XLA Ops:
  9.9 42.8 %psum.21 = f32[4096]{0:T(1024)S(1)} all-reduce(f32[4096]{0:T(1024)S(1)} %bitcast.117), channel_id=1, replica_groups=mesh['cluster'=4,'member'=8] {'cluster','member'}, use_global_device_ids=true, to_apply=%region_0.0 | all-reduce | flops 4096 | bytes 32768 | tf_op jit(solution)/shard_map/psum | solution.py:32
  52.8 22.7 %all-gather.6.cloned.1.call-done = bf16[4096,512]{1,0:T(8,128)(2,1)} async-done(((bf16[128,512]{1,0:T(8,128)(2,1)}), bf16[4096,512]{1,0:T(8,128)(2,1)}) %all-gather.6.cloned.1.call-update) | async-done | bytes 4194320 | tf_op jit(solution)/shard_map/all_gather | solution.py:13
  75.4 7.9 fusion.4
  83.4 153.1 %reduce-scatter.3.cloned.1.call-done = f32[128,512]{1,0:T(8,128)} async-done(((f32[4096,512]{1,0:T(8,128)}), f32[128,512]{1,0:T(8,128)}) %reduce-scatter.3.cloned.1.call-update) | async-done | bytes 262160 | tf_op jit(solution)/shard_map/reduce_scatter | solution.py:17
  240.5 129.6 %all-reduce.4.cloned.1.call-done = f32[512,512]{0,1:T(8,128)} async-done(((f32[512,512]{0,1:T(8,128)}), f32[512,512]{0,1:T(8,128)}) %all-reduce.4.cloned.1.call-update) | async-done | bytes 1048592 | tf_op jit(solution)/shard_map/psum | solution.py:42
  375.3 11.7 %cholesky.286 = f32[128,128]{1,0:T(8,128)S(1)} custom-call(f32[128,128]{1,0:T(8,128)S(1)} %cholesky.426), custom_call_target="Cholesky" | custom-call | tf_op jit(solution)/shard_map/jit(cholesky)/cholesky | solution.py:43
  387.5 9.8 custom-call.27
  400.7 11.7 %cholesky.305 = f32[128,128]{1,0:T(8,128)S(1)} custom-call(f32[128,128]{1,0:T(8,128)S(1)} %cholesky.430), custom_call_target="Cholesky" | custom-call | tf_op jit(solution)/shard_map/jit(cholesky)/cholesky | solution.py:43
  412.9 10.3 custom-call.28
  426.3 13.2 %cholesky.326 = f32[128,128]{1,0:T(8,128)} custom-call(f32[128,128]{1,0:T(8,128)} %cholesky.435), custom_call_target="Cholesky" | custom-call | tf_op jit(solution)/shard_map/jit(cholesky)/cholesky | solution.py:43
  441.6 11.3 custom-call.29
  455.1 11.7 %cholesky.343 = f32[128,128]{1,0:T(8,128)S(1)} custom-call(f32[128,128]{1,0:T(8,128)S(1)} %convolution_subtract_fusion.11), custom_call_target="Cholesky" | custom-call | tf_op jit(solution)/shard_map/jit(cholesky)/cholesky | solution.py:43
  472.6 12.0 %while.4 = (s32[]{:T(128)}, f32[512,512]{1,0:T(8,128)}, s32[4,2]{0,1:T(2,128)S(1)}, f32[4,128,128]{2,1,0:T(8,128)S(1)}, s32[]{:T(128)}) while((s32[]{:T(128)}, f32[512,512]{1,0:T(8,128)}, s32[4,2]{0,1:T(2,128)S(1)}, f32[4,128,128]{2,1,0:T(8,128)S(1)}, s32[]{:T(128)}) %tuple.59), condition=%wide.while_cond, body=%wide.while_body.sunk | while | flops 2 | bytes 131181 | solution.py:44
  485.2 39.3 %custom-call.30 = f32[4,128,128]{1,2,0:T(8,128)S(1)} custom-call(f32[4,128,128]{2,1,0:T(8,128)S(1)} %get-tuple-element.18), custom_call_target="InvertDiagBlocksLowerTriangular" | custom-call | tf_op jit(solution)/shard_map/jit(_solve_triangular)/triangular_solve | solution.py:44
  530.3 64.1 %all-gather.8.cloned.1.call-done = bf16[4096,512]{0,1:T(8,128)(2,1)} async-done(((bf16[128,512]{0,1:T(8,128)(2,1)}), bf16[4096,512]{0,1:T(8,128)(2,1)}) %all-gather.8.cloned.1.call-update) | async-done | bytes 4194320 | tf_op jit(solution)/shard_map/all_gather | solution.py:13
  594.5 7.9 fusion.2
  602.5 152.4 %reduce-scatter.5.cloned.1.call-done = f32[128,512]{1,0:T(8,128)} async-done(((f32[4096,512]{1,0:T(8,128)}), f32[128,512]{1,0:T(8,128)}) %reduce-scatter.5.cloned.1.call-update) | async-done | bytes 262160 | tf_op jit(solution)/shard_map/reduce_scatter | solution.py:17
  754.9 3.2 fusion.11
  758.4 130.1 %all-reduce.6.cloned.1.call-done = f32[512,512]{0,1:T(8,128)} async-done(((f32[512,512]{0,1:T(8,128)}), f32[512,512]{0,1:T(8,128)}) %all-reduce.6.cloned.1.call-update) | async-done | bytes 1048592 | tf_op jit(solution)/shard_map/psum | solution.py:42
  893.6 11.7 %cholesky.358 = f32[128,128]{1,0:T(8,128)S(1)} custom-call(f32[128,128]{1,0:T(8,128)S(1)} %cholesky.439), custom_call_target="Cholesky" | custom-call | tf_op jit(solution)/shard_map/jit(cholesky)/cholesky | solution.py:43
  906.1 9.8 custom-call.31
  919.1 11.7 %cholesky.377 = f32[128,128]{1,0:T(8,128)S(1)} custom-call(f32[128,128]{1,0:T(8,128)S(1)} %cholesky.443), custom_call_target="Cholesky" | custom-call | tf_op jit(solution)/shard_map/jit(cholesky)/cholesky | solution.py:43
  932.8 10.2 custom-call.32
  946.1 13.2 %cholesky.398 = f32[128,128]{1,0:T(8,128)} custom-call(f32[128,128]{1,0:T(8,128)} %cholesky.448), custom_call_target="Cholesky" | custom-call | tf_op jit(solution)/shard_map/jit(cholesky)/cholesky | solution.py:43
  961.5 11.3 custom-call.33
  975.0 12.3 %cholesky.415 = f32[128,128]{1,0:T(8,128)} custom-call(f32[128,128]{1,0:T(8,128)S(1)} %convolution_subtract_fusion.9), custom_call_target="Cholesky" | custom-call | tf_op jit(solution)/shard_map/jit(cholesky)/cholesky | solution.py:43
  992.7 11.6 %while.5 = (s32[]{:T(128)}, f32[512,512]{1,0:T(8,128)}, s32[4,2]{0,1:T(2,128)S(1)}, f32[4,128,128]{2,1,0:T(8,128)S(1)}, s32[]{:T(128)}) while((s32[]{:T(128)}, f32[512,512]{1,0:T(8,128)}, s32[4,2]{0,1:T(2,128)S(1)}, f32[4,128,128]{2,1,0:T(8,128)S(1)}, s32[]{:T(128)}) %tuple.81), condition=%wide.while_cond.clone, body=%wide.while_body.clone.sunk | while | flops 2 | bytes 131181 | solution.py:44
  1004.3 39.3 %custom-call.34 = f32[4,128,128]{1,2,0:T(8,128)S(1)} custom-call(f32[4,128,128]{2,1,0:T(8,128)S(1)} %get-tuple-element.19), custom_call_target="InvertDiagBlocksLowerTriangular" | custom-call | tf_op jit(solution)/shard_map/jit(_solve_triangular)/triangular_solve | solution.py:44
  1049.4 64.1 %all-gather.10.cloned.1.call-done = bf16[4096,512]{0,1:T(8,128)(2,1)} async-done(((bf16[128,512]{0,1:T(8,128)(2,1)}), bf16[4096,512]{0,1:T(8,128)(2,1)}) %all-gather.10.cloned.1.call-update) | async-done | bytes 4194320 | tf_op jit(solution)/shard_map/all_gather | solution.py:13
  1113.5 3.6 multiply_reduce_fusion
  1118.0 9.8 all-gather
  1129.4 16.0 %all-gather.12.cloned.1.call-done = bf16[2048,512]{1,0:T(8,128)(2,1)} async-done(((bf16[256,512]{1,0:T(8,128)(2,1)}), bf16[2048,512]{1,0:T(8,128)(2,1)}) %all-gather.12.cloned.1.call-update) | async-done | bytes 2097168 | tf_op jit(solution)/shard_map/all_gather | solution.py:55
  (144 shorter events, 89.2 us)
Async XLA Ops:
  7.2 68.3 %copy-start = (bf16[256,4096]{1,0:T(8,128)(2,1)S(1)}, bf16[256,4096]{1,0:T(8,128)(2,1)}, u32[]{:S(2)}) copy-start(bf16[256,4096]{1,0:T(8,128)(2,1)} %param.7) | copy-start | bytes 6291460
  7.2 68.3 %all-gather.6.cloned.1.call-start = ((), (), s32[]{:S(2)}) async-start(), calls=%async_computation.2 | async-start | bytes 4325376 | tf_op jit(solution)/shard_map/all_gather | solution.py:13
  7.9 228.5 %reduce-scatter.3.cloned.1.call-start = ((), (), s32[]{:S(2)}) async-start(), calls=%async_computation.3 | async-start | bytes 8650752 | tf_op jit(solution)/shard_map/reduce_scatter | solution.py:17
  83.3 286.8 %all-reduce.4.cloned.1.call-start = ((), (), s32[]{:S(2)}) async-start(), calls=%async_computation.4 | async-start | bytes 2097152 | tf_op jit(solution)/shard_map/psum | solution.py:42
  236.4 4.1 copy-start.5
  239.6 354.8 %all-gather.8.cloned.1.call-start = ((), (), s32[]{:S(2)}) async-start(), calls=%async_computation.5 | async-start | bytes 4325376 | tf_op jit(solution)/shard_map/all_gather | solution.py:13
  370.1 2.7 copy-start.1
  374.3 1.0 copy-start.4
  400.0 0.7 copy-start.8
  466.8 5.8 copy-start.12
  484.7 0.6 copy-start.9
  530.3 224.6 %reduce-scatter.5.cloned.1.call-start = ((), (), s32[]{:S(2)}) async-start(), calls=%async_computation.6 | async-start | bytes 8650752 | tf_op jit(solution)/shard_map/reduce_scatter | solution.py:17
  602.4 286.0 %all-reduce.6.cloned.1.call-start = ((), (), s32[]{:S(2)}) async-start(), calls=%async_computation.7 | async-start | bytes 2097152 | tf_op jit(solution)/shard_map/psum | solution.py:42
  754.9 3.5 copy-start.6
  758.1 355.5 %all-gather.10.cloned.1.call-start = ((), (), s32[]{:S(2)}) async-start(), calls=%async_computation.8 | async-start | bytes 4325376 | tf_op jit(solution)/shard_map/all_gather | solution.py:13
  888.5 2.7 copy-start.2
  892.6 1.0 copy-start.3
  918.4 0.7 copy-start.7
  973.8 18.9 %copy-start.10 = (s32[4,2]{0,1:T(2,128)S(1)}, s32[4,2]{0,1:T(2,128)}, u32[]{:S(2)}) copy-start(s32[4,2]{0,1:T(2,128)} %copy-done.9) | copy-start | bytes 100
  1049.3 68.6 %copy-start.11 = (s32[256]{0:T(256)S(1)}, s32[256]{0:T(256)}, u32[]{:S(2)}) copy-start(s32[256]{0:T(256)} %param.9) | copy-start | bytes 3076
  1049.3 96.1 %all-gather.12.cloned.1.call-start = ((), (), s32[]{:S(2)}) async-start(), calls=%async_computation.9 | async-start | bytes 2359296 | tf_op jit(solution)/shard_map/all_gather | solution.py:55
Sparse Core Ops, SparseCore 0:
  11.0 64.3 all-gather.5
  83.5 152.9 reduce-scatter.2
  241.6 128.4 all-reduce.3
  530.4 64.0 all-gather.7
  602.5 152.2 reduce-scatter.4
  759.9 128.4 all-reduce.5
  1049.4 64.0 all-gather.9
  1118.1 27.3 all-gather.11
where the time goes:
time: 1160 us
  waiting for transfers between devices  733 us (63%)
  other arithmetic  259 us (22%)
  matrix products  54.7 us (5%)
  blocking collectives  52.6 us (5%)
  local copies, waits for them, and re-layouts  35.1 us (3%)
  between operations  20.6 us (2%)
    reduce_scatter x2, waiting for transfers between devices, reduce_image(): lax.psum_scatter(lax.dot_general(centered, projected, (((0,), (0,)), ((),...  305 us
    psum x2, waiting for transfers between devices, body(): gram = lax.psum(local_gram, ('cluster', 'member'))  260 us
    another operation x29, other arithmetic, body(): lower = jnp.linalg.cholesky(gram)  172 us
    all_gather x3, waiting for transfers between devices, spread_basis(): return lax.all_gather(local_rows, ('cluster', 'member'), axis=0, tiled=True)  151 us
    another operation x5, other arithmetic, body(): jax.scipy.linalg.solve_triangular(lower, image.T, lower=True)  81.4 us
    psum x1, blocking collectives, body(): average = lax.psum(column_sums, ('cluster', 'member')) / total_rows  42.8 us
    another operation x27, local copies, waits for them, and re-layouts, body(): jax.scipy.linalg.solve_triangular(lower, image.T, lower=True)  23.5 us
  transfers between devices with their start and end apart: 8, of which 8 were waited for; matrix products, arithmetic and copies ran while one was open for 0% of the time, Pallas kernels for 0%

commit v1 on v0

--- a/solution.py
+++ b/solution.py
@@ -39,7 +39,8 @@
         )
         image = reduce_image(centered, projected) / total_rows
         local_gram = jnp.dot(image.T, image, precision=lax.Precision.HIGHEST)
-        gram = lax.psum(local_gram, ("cluster", "member"))
+        parts = lax.all_gather(local_gram, ("cluster", "member"), axis=0, tiled=False)
+        gram = parts.sum(axis=0)
         lower = jnp.linalg.cholesky(gram)
         orthonormal = jax.scipy.linalg.solve_triangular(lower, image.T, lower=True).T
         basis_full = spread_basis(orthonormal.astype(jnp.bfloat16))

time: 1160 us -> 1310 us (1.13)
  waiting for transfers between devices: 733 us -> 853 us
  other arithmetic: 259 us -> 284 us
    all_gather x0 -> x2, waiting for transfers between devices: none -> 382 us  [body(): lax.all_gather(local_gram, ('cluster', 'member'), axis=0, tiled=False)]
    psum x2 -> x0, waiting for transfers between devices: 260 us -> none  [body(): gram = lax.psum(local_gram, ('cluster', 'member'))]
    reduce_sum x0 -> x2, other arithmetic: none -> 25.4 us  [body(): gram = parts.sum(axis=0)]
where the time goes in v1:
time: 1310 us; the launch traced here: 1300 us
  waiting for transfers between devices  853 us (65%)
  other arithmetic  284 us (22%)
  matrix products  54.5 us (4%)
  blocking collectives  52.7 us (4%)
  local copies, waits for them, and re-layouts  36.2 us (3%)
  between operations  20.5 us (2%)
    all_gather x2, waiting for transfers between devices, body(): lax.all_gather(local_gram, ('cluster', 'member'), axis=0, tiled=False)  382 us
    reduce_scatter x2, waiting for transfers between devices, reduce_image(): lax.psum_scatter(lax.dot_general(centered, projected, (((0,), (0,)), ((),...  305 us
    another operation x29, other arithmetic, body(): lower = jnp.linalg.cholesky(gram)  170 us
    all_gather x3, waiting for transfers between devices, spread_basis(): return lax.all_gather(local_rows, ('cluster', 'member'), axis=0, tiled=True)  149 us
    another operation x5, other arithmetic, body(): jax.scipy.linalg.solve_triangular(lower, image.T, lower=True)  81.8 us
    psum x1, blocking collectives, body(): average = lax.psum(column_sums, ('cluster', 'member')) / total_rows  42.8 us
    another operation x27, local copies, waits for them, and re-layouts, body(): jax.scipy.linalg.solve_triangular(lower, image.T, lower=True)  27.3 us
  transfers between devices with their start and end apart: 8, of which 8 were waited for; matrix products, arithmetic and copies ran while one was open for 0% of the time, Pallas kernels for 0%

profile of v1, /device:TPU:0, one launch (start us, length us, event | category | flops | bytes accessed | tf_op | source)
XLA Modules:
  0.0 1301.4 jit_solution(2009084249995780442)
XLA Ops:
  9.9 42.8 %psum.7 = f32[4096]{0:T(1024)S(1)} all-reduce(f32[4096]{0:T(1024)S(1)} %bitcast.121), channel_id=1, replica_groups=mesh['cluster'=4,'member'=8] {'cluster','member'}, use_global_device_ids=true, to_apply=%region_0.0 | all-reduce | flops 4096 | bytes 32768 | tf_op jit(solution)/shard_map/psum | solution.py:32
  52.8 22.7 %all-gather.10.cloned.1.call-done = bf16[4096,512]{1,0:T(8,128)(2,1)} async-done(((bf16[128,512]{1,0:T(8,128)(2,1)}), bf16[4096,512]{1,0:T(8,128)(2,1)}) %all-gather.10.cloned.1.call-update) | async-done | bytes 4194320 | tf_op jit(solution)/shard_map/all_gather | solution.py:13
  75.4 7.9 fusion.4
  83.4 152.3 %reduce-scatter.3.cloned.1.call-done = f32[128,512]{1,0:T(8,128)} async-done(((f32[4096,512]{1,0:T(8,128)}), f32[128,512]{1,0:T(8,128)}) %reduce-scatter.3.cloned.1.call-update) | async-done | bytes 262160 | tf_op jit(solution)/shard_map/reduce_scatter | solution.py:17
  240.3 190.7 %all-gather.18.cloned.1.call-done = f32[16384,512]{1,0:T(8,128)} async-done(((f32[512,512]{1,0:T(8,128)}), f32[16384,512]{1,0:T(8,128)}) %all-gather.18.cloned.1.call-update) | async-done | bytes 33554448 | tf_op jit(solution)/shard_map/all_gather | solution.py:42
  431.0 12.7 reduce_sum.27
  447.5 11.7 cholesky.286
  459.8 9.8 custom-call.27
  472.9 11.7 cholesky.305
  485.2 9.9 custom-call.28
  498.3 13.2 %cholesky.326 = f32[128,128]{1,0:T(8,128)} custom-call(f32[128,128]{1,0:T(8,128)} %cholesky.435), custom_call_target="Cholesky" | custom-call | tf_op jit(solution)/shard_map/jit(cholesky)/cholesky | solution.py:44
  513.6 11.3 custom-call.29
  527.2 11.7 cholesky.343
  545.4 12.0 while.4
  558.0 39.3 %custom-call.30 = f32[4,128,128]{1,2,0:T(8,128)S(1)} custom-call(f32[4,128,128]{2,1,0:T(8,128)S(1)} %get-tuple-element.18), custom_call_target="InvertDiagBlocksLowerTriangular" | custom-call | tf_op jit(solution)/shard_map/jit(_solve_triangular)/triangular_solve | solution.py:45
  603.1 63.4 %all-gather.12.cloned.1.call-done = bf16[4096,512]{0,1:T(8,128)(2,1)} async-done(((bf16[128,512]{0,1:T(8,128)(2,1)}), bf16[4096,512]{0,1:T(8,128)(2,1)}) %all-gather.12.cloned.1.call-update) | async-done | bytes 4194320 | tf_op jit(solution)/shard_map/all_gather | solution.py:13
  666.5 7.9 fusion.2
  674.5 152.6 %reduce-scatter.5.cloned.1.call-done = f32[128,512]{1,0:T(8,128)} async-done(((f32[4096,512]{1,0:T(8,128)}), f32[128,512]{1,0:T(8,128)}) %reduce-scatter.5.cloned.1.call-update) | async-done | bytes 262160 | tf_op jit(solution)/shard_map/reduce_scatter | solution.py:17
  831.2 190.9 %all-gather.20.cloned.1.call-done = f32[16384,512]{1,0:T(8,128)} async-done(((f32[512,512]{1,0:T(8,128)}), f32[16384,512]{1,0:T(8,128)}) %all-gather.20.cloned.1.call-update) | async-done | bytes 33554448 | tf_op jit(solution)/shard_map/all_gather | solution.py:42
  1022.1 12.7 reduce_sum.28
  1038.5 11.7 cholesky.358
  1051.0 9.8 custom-call.31
  1064.0 11.7 cholesky.377
  1077.8 9.9 custom-call.32
  1090.8 13.2 %cholesky.398 = f32[128,128]{1,0:T(8,128)} custom-call(f32[128,128]{1,0:T(8,128)} %cholesky.448), custom_call_target="Cholesky" | custom-call | tf_op jit(solution)/shard_map/jit(cholesky)/cholesky | solution.py:44
  1106.2 11.3 custom-call.33
  1119.7 11.7 cholesky.415
  1136.0 14.8 %while.5 = (s32[]{:T(128)}, f32[512,512]{1,0:T(8,128)}, s32[4,2]{0,1:T(2,128)}, f32[4,128,128]{2,1,0:T(8,128)S(1)}, s32[]{:T(128)}) while((s32[]{:T(128)}, f32[512,512]{1,0:T(8,128)}, s32[4,2]{0,1:T(2,128)}, f32[4,128,128]{2,1,0:T(8,128)S(1)}, s32[]{:T(128)}) %tuple.81), condition=%wide.while_cond.clone, body=%wide.while_body.clone.sunk | while | flops 2 | bytes 131181 | solution.py:45
  1150.7 39.3 %custom-call.34 = f32[4,128,128]{1,2,0:T(8,128)S(1)} custom-call(f32[4,128,128]{2,1,0:T(8,128)S(1)} %get-tuple-element.19), custom_call_target="InvertDiagBlocksLowerTriangular" | custom-call | tf_op jit(solution)/shard_map/jit(_solve_triangular)/triangular_solve | solution.py:45
  1195.8 63.4 %all-gather.14.cloned.1.call-done = bf16[4096,512]{0,1:T(8,128)(2,1)} async-done(((bf16[128,512]{0,1:T(8,128)(2,1)}), bf16[4096,512]{0,1:T(8,128)(2,1)}) %all-gather.14.cloned.1.call-update) | async-done | bytes 4194320 | tf_op jit(solution)/shard_map/all_gather | solution.py:13
  1263.6 9.8 all-gather.2
  1275.1 16.0 %all-gather.16.cloned.1.call-done = bf16[2048,512]{1,0:T(8,128)(2,1)} async-done(((bf16[256,512]{1,0:T(8,128)(2,1)}), bf16[2048,512]{1,0:T(8,128)(2,1)}) %all-gather.16.cloned.1.call-update) | async-done | bytes 2097168 | tf_op jit(solution)/shard_map/all_gather | solution.py:56
  (134 shorter events, 97.7 us)
Async XLA Ops:
  7.2 68.3 %copy-start = (bf16[256,4096]{1,0:T(8,128)(2,1)S(1)}, bf16[256,4096]{1,0:T(8,128)(2,1)}, u32[]{:S(2)}) copy-start(bf16[256,4096]{1,0:T(8,128)(2,1)} %param.7) | copy-start | bytes 6291460
  7.2 68.3 %all-gather.10.cloned.1.call-start = ((), (), s32[]{:S(2)}) async-start(), calls=%async_computation.2 | async-start | bytes 4325376 | tf_op jit(solution)/shard_map/all_gather | solution.py:13
  7.9 227.8 %reduce-scatter.3.cloned.1.call-start = ((), (), s32[]{:S(2)}) async-start(), calls=%async_computation.3 | async-start | bytes 8650752 | tf_op jit(solution)/shard_map/reduce_scatter | solution.py:17
  83.3 347.7 %all-gather.18.cloned.1.call-start = ((), (), s32[]{:S(2)}) async-start(), calls=%async_computation.8 | async-start | bytes 34603008 | tf_op jit(solution)/shard_map/all_gather | solution.py:42
  238.8 427.7 %all-gather.12.cloned.1.call-start = ((), (), s32[]{:S(2)}) async-start(), calls=%async_computation.4 | async-start | bytes 4325376 | tf_op jit(solution)/shard_map/all_gather | solution.py:13
  446.5 1.0 copy-start.2
  472.2 0.7 copy-start.4
  557.5 0.6 copy-start.5
  603.1 224.0 %reduce-scatter.5.cloned.1.call-start = ((), (), s32[]{:S(2)}) async-start(), calls=%async_computation.5 | async-start | bytes 8650752 | tf_op jit(solution)/shard_map/reduce_scatter | solution.py:17
  674.4 347.6 %all-gather.20.cloned.1.call-start = ((), (), s32[]{:S(2)}) async-start(), calls=%async_computation.9 | async-start | bytes 34603008 | tf_op jit(solution)/shard_map/all_gather | solution.py:42
  830.2 429.0 %all-gather.14.cloned.1.call-start = ((), (), s32[]{:S(2)}) async-start(), calls=%async_computation.6 | async-start | bytes 4325376 | tf_op jit(solution)/shard_map/all_gather | solution.py:13
  1037.5 1.0 copy-start.1
  1063.3 0.7 copy-start.3
  1195.8 67.9 %copy-start.6 = (s32[256]{0:T(256)S(1)}, s32[256]{0:T(256)}, u32[]{:S(2)}) copy-start(s32[256]{0:T(256)} %param.9) | copy-start | bytes 3076
  1195.8 95.3 %all-gather.16.cloned.1.call-start = ((), (), s32[]{:S(2)}) async-start(), calls=%async_computation.7 | async-start | bytes 2359296 | tf_op jit(solution)/shard_map/all_gather | solution.py:56
Sparse Core Ops, SparseCore 0:
  11.0 64.3 all-gather.9
  83.5 152.1 reduce-scatter.2
  238.9 192.0 all-gather.17
  603.2 63.2 all-gather.11
  674.6 152.4 reduce-scatter.4
  830.3 191.7 all-gather.19
  1195.9 63.2 all-gather.13
  1263.7 27.3 all-gather.15
